TPU v7x, 32 devices: a whole 2x2x4 slice. The times are simulated.
32 devices in a mesh: lat: 4 (over y, x), lon: 4 (over z), lev: 2 (over core).
Axes of the slice: x: 2, y: 2, z: 4, core: 2. Of those that a mesh axis runs over, the one named last changes fastest.
Arguments:
- field_values: float32 [16, 256, 192, 128], P('lat', 'lon', 'lev'), may hold values from 0.2 to 1.8
- crowding: float32 [16, 256, 192, 128], P('lat', 'lon', 'lev'), may hold values from 0.5 to 2
Outputs:
- field_values_end: float32 [16, 256, 192, 128], P('lat', 'lon', 'lev')
All inputs are finite; a program needn't handle non-finite values.
Results may differ from a plain program's by a relative error of at most 0.00002.
Values sent between devices are 32-bit elements; how exact they have to be, the bound alone decides.
A program may use at most 384 MiB of HBM per device.

v0:
```python
import jax
import jax.numpy as jnp
from jax import lax
from jax.sharding import PartitionSpec as P

STEPS = 3


def padded_2(block, sides, width):
    for axis, dim in sides:
        count = lax.axis_size(axis)
        forward = [(i, i + 1) for i in range(count - 1)]
        forward.append((count - 1, 0))
        backward = [(target, source) for source, target in forward]
        low = lax.ppermute(
            lax.slice_in_dim(block, block.shape[dim] - width, None, axis=dim), axis, forward
        )
        high = lax.ppermute(lax.slice_in_dim(block, 0, width, axis=dim), axis, backward)
        block = jnp.concatenate([low, block, high], axis=dim)
    return block


def without_rim(values, dims):
    for dim in dims:
        values = lax.slice_in_dim(values, 1, values.shape[dim] - 1, axis=dim)
    return values


def shifted_cells(values, dim, start, dims):
    others = [other for other in dims if other != dim]
    values = without_rim(values, others)
    return lax.slice_in_dim(values, start, start + values.shape[dim] - 2, axis=dim)


def march_step(padded, crowding):
    middle = without_rim(padded, (0, 1, 2))
    lower = [shifted_cells(padded, dim, 0, (0, 1, 2)) for dim in (0, 1, 2)]
    upper = [shifted_cells(padded, dim, 2, (0, 1, 2)) for dim in (0, 1, 2)]
    spread = lower[0] + upper[0] + lower[1] + upper[1] + lower[2] + upper[2] - 6.0 * middle
    return middle + 0.1 * spread + 0.2 * middle * (1.0 - middle * crowding)


def local(field_values, crowding):
    for step in range(STEPS):
        padded = padded_2(field_values, (("lat", 0), ("lon", 1), ("lev", 2)), 1)
        field_values = march_step(padded, crowding)
    return field_values


def solution(mesh):
    placed = (P("lat", "lon", "lev", None), P("lat", "lon", "lev", None))
    return jax.shard_map(
        local, mesh=mesh, in_specs=placed, out_specs=P("lat", "lon", "lev", None), check_vma=False
    )
```

profile of v0, /device:TPU:0, one launch (start us, length us, event | category | flops | bytes accessed | tf_op | source)
XLA Modules:
  0.0 624.0 jit_solution(13915528007051260947)
XLA Ops:
  0.0 5.0 fusion.30
  5.0 3.0 collective-permute-start
  7.9 1.0 collective-permute-start.1
  8.9 68.9 %collective-permute-done = f32[1,64,96,128]{3,2,1,0:T(8,128)S(1)} collective-permute-done((f32[1,64,96,128]{3,2,1,0:T(8,128)S(1)}, f32[1,64,96,128]{3,2,1,0:T(8,128)S(1)}, u32[]{:S(2)}, u32[]{:S(2)}) %collective-permute-start) | collective-permute-done | bytes 3145760 | tf_op jit(solution)/shard_map/ppermute | solution.py:15
  77.8 1.8 constant_dynamic-update-slice_fusion.2
  79.7 10.3 %constant_dynamic-update-slice_fusion.1 = f32[6,64,96,128]{3,2,1,0:T(8,128)} fusion(f32[6,64,96,128]{3,2,1,0:T(8,128)} %constant_dynamic-update-slice_fusion.2, f32[4,64,96,128]{3,2,1,0:T(8,128)} %param.2), kind=kLoop, calls=%fused_computation.93 | loop fusion | bytes 25165824
  90.0 54.6 %collective-permute-done.1 = f32[1,64,96,128]{3,2,1,0:T(8,128)S(1)} collective-permute-done((f32[1,64,96,128]{3,2,1,0:T(8,128)}, f32[1,64,96,128]{3,2,1,0:T(8,128)S(1)}, u32[]{:S(2)}, u32[]{:S(2)}) %collective-permute-start.1) | collective-permute-done | bytes 3145760 | tf_op jit(solution)/shard_map/ppermute | solution.py:18
  144.6 2.0 constant_dynamic-update-slice_fusion
  146.6 1.2 fusion.27
  147.8 1.6 collective-permute-start.2
  149.5 2.2 collective-permute-start.3
  151.7 7.9 %collective-permute-done.2 = f32[6,1,96,128]{3,2,1,0:T(8,128)S(1)} collective-permute-done((f32[6,1,96,128]{3,2,1,0:T(8,128)S(1)}, f32[6,1,96,128]{3,2,1,0:T(8,128)S(1)}, u32[]{:S(2)}, u32[]{:S(2)}) %collective-permute-start.2) | collective-permute-done | bytes 294944 | tf_op jit(solution)/shard_map/ppermute | solution.py:15
  159.6 3.8 collective-permute-done.3
  163.4 2.3 pad_maximum_fusion.64
  165.7 0.0 copy-done.4
  165.7 0.0 copy-done.5
  165.8 0.1 collective-permute-start.5
  165.9 0.6 collective-permute-start.4
  166.4 0.9 collective-permute-done.5
  167.3 0.9 copy.19
  168.2 0.0 collective-permute-done.4
  168.2 0.9 copy.17
  169.1 42.6 %fusion.22 = f32[4,64,96,128]{3,2,1,0:T(8,128)} fusion(f32[4,64,96,128]{3,2,1,0:T(8,128)} %param.2, f32[6,66,1,128]{3,2,1,0:T(1,128)} %copy.19, f32[6,1,96,128]{3,2,1,0:T(8,128)} %copy-done.5, f32[6,64,96,128]{3,2,1,0:T(8,128)} %constant_dynamic-update-slice_fusion, f32[6,1,96,128]{3,2,1,0:T(8,128)S(1)} %collective-permute-done.2, ...), kind=kLoop, calls=%fused_computation.59 | loop fusion | flops 75497472 | bytes 63909888 | tf_op jit(solution)/shard_map/add | solution.py:40
  211.7 0.0 copy-start
  211.7 3.4 fusion.29
  215.2 1.5 collective-permute-start.6
  216.7 1.4 collective-permute-start.7
  218.2 68.9 %collective-permute-done.6 = f32[1,64,96,128]{3,2,1,0:T(8,128)S(1)} collective-permute-done((f32[1,64,96,128]{3,2,1,0:T(8,128)S(1)}, f32[1,64,96,128]{3,2,1,0:T(8,128)S(1)}, u32[]{:S(2)}, u32[]{:S(2)}) %collective-permute-start.6) | collective-permute-done | bytes 3145760 | tf_op jit(solution)/shard_map/ppermute | solution.py:15
  287.1 65.6 %collective-permute-done.7 = f32[1,64,96,128]{3,2,1,0:T(8,128)S(1)} collective-permute-done((f32[1,64,96,128]{3,2,1,0:T(8,128)S(1)}, f32[1,64,96,128]{3,2,1,0:T(8,128)S(1)}, u32[]{:S(2)}, u32[]{:S(2)}) %collective-permute-start.7) | collective-permute-done | bytes 3145760 | tf_op jit(solution)/shard_map/ppermute | solution.py:18
  352.7 0.0 copy-done
  352.8 1.2 collective-permute-start.8
  354.0 2.7 collective-permute-start.9
  356.7 7.9 %collective-permute-done.8 = f32[6,1,96,128]{3,2,1,0:T(8,128)S(1)} collective-permute-done((f32[6,1,96,128]{3,2,1,0:T(8,128)S(1)}, f32[6,1,96,128]{3,2,1,0:T(8,128)S(1)}, u32[]{:S(2)}, u32[]{:S(2)}) %collective-permute-start.8) | collective-permute-done | bytes 294944 | tf_op jit(solution)/shard_map/ppermute | solution.py:15
  364.5 3.7 collective-permute-done.9
  368.2 0.3 pad_maximum_fusion.61
  368.5 0.0 copy-done.2
  368.5 0.4 copy-done.6
  368.9 0.1 collective-permute-start.11
  369.0 0.6 collective-permute-start.10
  369.6 0.9 collective-permute-done.11
  370.5 0.9 copy.23
  371.4 0.0 collective-permute-done.10
  371.4 0.9 copy.21
  372.3 45.2 %fusion.13 = f32[4,64,96,128]{3,2,1,0:T(8,128)} fusion(f32[4,64,96,128]{3,2,1,0:T(8,128)} %fusion.22, f32[6,66,1,128]{3,2,1,0:T(1,128)} %copy.23, f32[6,1,96,128]{3,2,1,0:T(8,128)} %copy-done.6, f32[6,1,96,128]{3,2,1,0:T(8,128)S(1)} %collective-permute-done.8, f32[1,64,96,128]{3,2,1,0:T(8,128)} %copy-done.2, ...), kind=kLoop, calls=%fused_computation.32 | loop fusion | flops 100663296 | bytes 45035520 | tf_op jit(solution)/shard_map/add | solution.py:40
  417.4 0.0 copy-start.1
  417.4 3.4 fusion.28
  420.9 1.5 collective-permute-start.12
  422.4 1.5 collective-permute-start.13
  423.9 68.9 %collective-permute-done.12 = f32[1,64,96,128]{3,2,1,0:T(8,128)S(1)} collective-permute-done((f32[1,64,96,128]{3,2,1,0:T(8,128)S(1)}, f32[1,64,96,128]{3,2,1,0:T(8,128)S(1)}, u32[]{:S(2)}, u32[]{:S(2)}) %collective-permute-start.12) | collective-permute-done | bytes 3145760 | tf_op jit(solution)/shard_map/ppermute | solution.py:15
  492.8 66.6 %collective-permute-done.13 = f32[1,64,96,128]{3,2,1,0:T(8,128)S(1)} collective-permute-done((f32[1,64,96,128]{3,2,1,0:T(8,128)S(1)}, f32[1,64,96,128]{3,2,1,0:T(8,128)S(1)}, u32[]{:S(2)}, u32[]{:S(2)}) %collective-permute-start.13) | collective-permute-done | bytes 3145760 | tf_op jit(solution)/shard_map/ppermute | solution.py:18
  559.4 0.0 copy-done.1
  559.5 0.8 collective-permute-start.14
  560.3 3.1 collective-permute-start.15
  563.4 7.9 %collective-permute-done.14 = f32[6,1,96,128]{3,2,1,0:T(8,128)S(1)} collective-permute-done((f32[6,1,96,128]{3,2,1,0:T(8,128)S(1)}, f32[6,1,96,128]{3,2,1,0:T(8,128)S(1)}, u32[]{:S(2)}, u32[]{:S(2)}) %collective-permute-start.14) | collective-permute-done | bytes 294944 | tf_op jit(solution)/shard_map/ppermute | solution.py:15
  571.2 3.3 collective-permute-done.15
  574.5 0.3 pad_maximum_fusion.56
  574.8 0.4 copy-done.7
  575.2 0.1 collective-permute-start.17
  575.3 0.6 collective-permute-start.16
  575.9 0.9 collective-permute-done.17
  576.8 0.9 copy.27
  577.7 0.0 collective-permute-done.16
  577.7 0.9 copy.25
  578.6 45.2 %fusion.4 = f32[4,64,96,128]{3,2,1,0:T(8,128)} fusion(f32[4,64,96,128]{3,2,1,0:T(8,128)} %fusion.13, f32[6,66,1,128]{3,2,1,0:T(1,128)} %copy.27, f32[6,1,96,128]{3,2,1,0:T(8,128)} %copy-done.7, f32[6,1,96,128]{3,2,1,0:T(8,128)S(1)} %collective-permute-done.14, f32[1,64,96,128]{3,2,1,0:T(8,128)} %copy-done.3, ...), kind=kLoop, calls=%fused_computation.5 | loop fusion | flops 100663296 | bytes 45035520 | tf_op jit(solution)/shard_map/add | solution.py:40
  (15 shorter events, 0.2 us)
Async XLA Ops:
  5.0 72.9 %collective-permute-start = (f32[1,64,96,128]{3,2,1,0:T(8,128)S(1)}, f32[1,64,96,128]{3,2,1,0:T(8,128)S(1)}, u32[]{:S(2)}, u32[]{:S(2)}) collective-permute-start(f32[1,64,96,128]{3,2,1,0:T(8,128)S(1)} %get-tuple-element.22), channel_id=1, source_target_pairs={{0,8},{8,16},{16,24},{24,0},{1,9},{9,17},{17,25},{25,1},{2,10},{10... | collective-permute-start | bytes 9437192 | tf_op jit(solution)/shard_map/ppermute | solution.py:15
  7.9 136.7 %collective-permute-start.1 = (f32[1,64,96,128]{3,2,1,0:T(8,128)}, f32[1,64,96,128]{3,2,1,0:T(8,128)S(1)}, u32[]{:S(2)}, u32[]{:S(2)}) collective-permute-start(f32[1,64,96,128]{3,2,1,0:T(8,128)} %get-tuple-element.21), channel_id=1, source_target_pairs={{8,0},{16,8},{24,16},{0,24},{9,1},{17,9},{25,17},{1,25},{10,2},{18... | collective-permute-start | bytes 9437192 | tf_op jit(solution)/shard_map/ppermute | solution.py:18
  144.6 21.1 %copy-start.4 = (f32[1,64,96,128]{3,2,1,0:T(8,128)}, f32[1,64,96,128]{3,2,1,0:T(8,128)S(1)}, u32[]{:S(2)}) copy-start(f32[1,64,96,128]{3,2,1,0:T(8,128)S(1)} %collective-permute-done.1) | copy-start | bytes 9437188
  147.8 11.8 %collective-permute-start.2 = (f32[6,1,96,128]{3,2,1,0:T(8,128)S(1)}, f32[6,1,96,128]{3,2,1,0:T(8,128)S(1)}, u32[]{:S(2)}, u32[]{:S(2)}) collective-permute-start(f32[6,1,96,128]{3,2,1,0:T(8,128)S(1)} %get-tuple-element.15), channel_id=1, source_target_pairs={{0,2},{2,4},{4,6},{6,0},{1,3},{3,5},{5,7},{7,1},{8,10},{10,12},{12... | collective-permute-start | bytes 884744 | tf_op jit(solution)/shard_map/ppermute | solution.py:15
  149.5 13.9 %collective-permute-start.3 = (f32[6,1,96,128]{3,2,1,0:T(8,128)S(1)}, f32[6,1,96,128]{3,2,1,0:T(8,128)S(1)}, u32[]{:S(2)}, u32[]{:S(2)}) collective-permute-start(f32[6,1,96,128]{3,2,1,0:T(8,128)S(1)} %get-tuple-element.16), channel_id=1, source_target_pairs={{2,0},{4,2},{6,4},{0,6},{3,1},{5,3},{7,5},{1,7},{10,8},{12,10},{14... | collective-permute-start | bytes 884744 | tf_op jit(solution)/shard_map/ppermute | solution.py:18
  163.4 2.3 copy-start.5
  165.8 1.5 collective-permute-start.5
  165.9 2.3 collective-permute-start.4
  211.7 141.0 %copy-start = (f32[4,64,96,128]{3,2,1,0:T(8,128)S(1)}, f32[4,64,96,128]{3,2,1,0:T(8,128)}, u32[]{:S(2)}) copy-start(f32[4,64,96,128]{3,2,1,0:T(8,128)} %fusion.22) | copy-start | bytes 37748740
  215.2 71.9 %collective-permute-start.6 = (f32[1,64,96,128]{3,2,1,0:T(8,128)S(1)}, f32[1,64,96,128]{3,2,1,0:T(8,128)S(1)}, u32[]{:S(2)}, u32[]{:S(2)}) collective-permute-start(f32[1,64,96,128]{3,2,1,0:T(8,128)S(1)} %get-tuple-element.19), channel_id=1, source_target_pairs={{0,8},{8,16},{16,24},{24,0},{1,9},{9,17},{17,25},{25,1},{2,10},{10... | collective-permute-start | bytes 9437192 | tf_op jit(solution)/shard_map/ppermute | solution.py:15
  216.7 136.0 %collective-permute-start.7 = (f32[1,64,96,128]{3,2,1,0:T(8,128)S(1)}, f32[1,64,96,128]{3,2,1,0:T(8,128)S(1)}, u32[]{:S(2)}, u32[]{:S(2)}) collective-permute-start(f32[1,64,96,128]{3,2,1,0:T(8,128)S(1)} %get-tuple-element.20), channel_id=1, source_target_pairs={{8,0},{16,8},{24,16},{0,24},{9,1},{17,9},{25,17},{1,25},{10,2},{18... | collective-permute-start | bytes 9437192 | tf_op jit(solution)/shard_map/ppermute | solution.py:18
  352.7 15.8 %copy-start.2 = (f32[1,64,96,128]{3,2,1,0:T(8,128)}, f32[1,64,96,128]{3,2,1,0:T(8,128)S(1)}, u32[]{:S(2)}) copy-start(f32[1,64,96,128]{3,2,1,0:T(8,128)S(1)} %collective-permute-done.7) | copy-start | bytes 9437188
  352.8 11.7 %collective-permute-start.8 = (f32[6,1,96,128]{3,2,1,0:T(8,128)S(1)}, f32[6,1,96,128]{3,2,1,0:T(8,128)S(1)}, u32[]{:S(2)}, u32[]{:S(2)}) collective-permute-start(f32[6,1,96,128]{3,2,1,0:T(8,128)S(1)} %get-tuple-element.13), channel_id=1, source_target_pairs={{0,2},{2,4},{4,6},{6,0},{1,3},{3,5},{5,7},{7,1},{8,10},{10,12},{12... | collective-permute-start | bytes 884744 | tf_op jit(solution)/shard_map/ppermute | solution.py:15
  354.0 14.2 %collective-permute-start.9 = (f32[6,1,96,128]{3,2,1,0:T(8,128)S(1)}, f32[6,1,96,128]{3,2,1,0:T(8,128)S(1)}, u32[]{:S(2)}, u32[]{:S(2)}) collective-permute-start(f32[6,1,96,128]{3,2,1,0:T(8,128)S(1)} %get-tuple-element.14), channel_id=1, source_target_pairs={{2,0},{4,2},{6,4},{0,6},{3,1},{5,3},{7,5},{1,7},{10,8},{12,10},{14... | collective-permute-start | bytes 884744 | tf_op jit(solution)/shard_map/ppermute | solution.py:18
  368.2 0.7 copy-start.6
  368.9 1.5 collective-permute-start.11
  369.0 2.4 collective-permute-start.10
  417.4 142.0 %copy-start.1 = (f32[4,64,96,128]{3,2,1,0:T(8,128)S(1)}, f32[4,64,96,128]{3,2,1,0:T(8,128)}, u32[]{:S(2)}) copy-start(f32[4,64,96,128]{3,2,1,0:T(8,128)} %fusion.13) | copy-start | bytes 37748740
  420.9 71.9 %collective-permute-start.12 = (f32[1,64,96,128]{3,2,1,0:T(8,128)S(1)}, f32[1,64,96,128]{3,2,1,0:T(8,128)S(1)}, u32[]{:S(2)}, u32[]{:S(2)}) collective-permute-start(f32[1,64,96,128]{3,2,1,0:T(8,128)S(1)} %get-tuple-element.17), channel_id=1, source_target_pairs={{0,8},{8,16},{16,24},{24,0},{1,9},{9,17},{17,25},{25,1},{2,10},{10... | collective-permute-start | bytes 9437192 | tf_op jit(solution)/shard_map/ppermute | solution.py:15
  422.4 137.0 %collective-permute-start.13 = (f32[1,64,96,128]{3,2,1,0:T(8,128)S(1)}, f32[1,64,96,128]{3,2,1,0:T(8,128)S(1)}, u32[]{:S(2)}, u32[]{:S(2)}) collective-permute-start(f32[1,64,96,128]{3,2,1,0:T(8,128)S(1)} %get-tuple-element.18), channel_id=1, source_target_pairs={{8,0},{16,8},{24,16},{0,24},{9,1},{17,9},{25,17},{1,25},{10,2},{18... | collective-permute-start | bytes 9437192 | tf_op jit(solution)/shard_map/ppermute | solution.py:18
  559.4 15.4 %copy-start.3 = (f32[1,64,96,128]{3,2,1,0:T(8,128)}, f32[1,64,96,128]{3,2,1,0:T(8,128)S(1)}, u32[]{:S(2)}) copy-start(f32[1,64,96,128]{3,2,1,0:T(8,128)S(1)} %collective-permute-done.13) | copy-start | bytes 9437188
  559.5 11.7 %collective-permute-start.14 = (f32[6,1,96,128]{3,2,1,0:T(8,128)S(1)}, f32[6,1,96,128]{3,2,1,0:T(8,128)S(1)}, u32[]{:S(2)}, u32[]{:S(2)}) collective-permute-start(f32[6,1,96,128]{3,2,1,0:T(8,128)S(1)} %get-tuple-element.11), channel_id=1, source_target_pairs={{0,2},{2,4},{4,6},{6,0},{1,3},{3,5},{5,7},{7,1},{8,10},{10,12},{12... | collective-permute-start | bytes 884744 | tf_op jit(solution)/shard_map/ppermute | solution.py:15
  560.3 14.2 %collective-permute-start.15 = (f32[6,1,96,128]{3,2,1,0:T(8,128)S(1)}, f32[6,1,96,128]{3,2,1,0:T(8,128)S(1)}, u32[]{:S(2)}, u32[]{:S(2)}) collective-permute-start(f32[6,1,96,128]{3,2,1,0:T(8,128)S(1)} %get-tuple-element.12), channel_id=1, source_target_pairs={{2,0},{4,2},{6,4},{0,6},{3,1},{5,3},{7,5},{1,7},{10,8},{12,10},{14... | collective-permute-start | bytes 884744 | tf_op jit(solution)/shard_map/ppermute | solution.py:18
  574.5 0.7 copy-start.7
  575.2 1.5 collective-permute-start.17
  575.3 2.4 collective-permute-start.16
where the time goes:
time: 624 us
  waiting for transfers between devices  431 us (69%)
  other arithmetic  136 us (22%)
  local copies, waits for them, and re-layouts  33.5 us (5%)
  starting transfers between devices  23.4 us (4%)
    ppermute x9, waiting for transfers between devices, padded_2(): lax.ppermute(lax.slice_in_dim(block, block.shape[dim] - width, None, axis...  230 us
    ppermute x9, waiting for transfers between devices, padded_2(): lax.ppermute(lax.slice_in_dim(block, 0, width, axis=dim), axis, backward)  200 us
    add x3, other arithmetic, march_step(): return middle + 0.1 * spread + 0.2 * middle * (1.0 - middle * crowding)  133 us
    unnamed x18, local copies, waits for them, and re-layouts  13 us
  transfers between devices with their start and end apart: 18, of which 15 were waited for; matrix products, arithmetic and copies ran while one was open for 2% of the time, Pallas kernels for 0%

commit v1 on v0

v1 whole, which is shorter than its diff:
```python
import functools
import math

import jax
import jax.numpy as jnp
from jax import lax
from jax.experimental import pallas as pl
from jax.experimental.pallas import tpu as pltpu
from jax.sharding import PartitionSpec as P

STEPS = 3
CHUNK_ROWS = 8
MESH = pl.DeviceIdType.MESH
AXES = ("lat", "lon", "lev")


def march_kernel(sizes, shape, rows, f_in, c_in, out, even, odd, crowd, jh, kh, kf,
                 load_sems, j_send, j_recv, i_send, i_recv, k_send, k_recv, out_sems):
    J, I, K, L = shape
    chunks = I // rows
    near = {}
    for axis, count in zip(AXES, sizes):
        me = lax.axis_index(axis)
        near[axis] = (lax.rem(me + count - 1, count), lax.rem(me + 1, count))

    barrier = pltpu.get_barrier_semaphore()
    for axis in AXES:
        for target in near[axis]:
            pl.semaphore_signal(barrier, inc=1, device_id={axis: target}, device_id_type=MESH)
    pl.semaphore_wait(barrier, 2 * len(AXES))

    fields = (even, odd)

    def remote(source, target, send, recv, axis, side):
        return pltpu.make_async_remote_copy(
            src_ref=source, dst_ref=target, send_sem=send, recv_sem=recv,
            device_id={axis: near[axis][side]}, device_id_type=MESH)

    def j_copy(step, side, chunk):
        j = (J - 1) * side
        if step == 0:
            source = f_in.at[j, pl.ds(chunk * rows, rows)]
        else:
            source = fields[step % 2].at[j, pl.ds(1 + chunk * rows, rows)]
        return remote(source, jh.at[step, 1 - side, pl.ds(chunk * rows, rows)],
                      j_send.at[step, side, chunk], j_recv.at[step, 1 - side, chunk], "lat", side)

    def i_copy(step, side):
        if step == 0:
            source = f_in.at[:, (I - 1) * side]
        else:
            source = fields[step % 2].at[:, 1 + (I - 1) * side]
        return remote(source, fields[step % 2].at[:, (I + 1) * (1 - side)],
                      i_send.at[step, side], i_recv.at[step, 1 - side], "lon", side)

    def k_copy(step, side):
        return remote(kf.at[step, side], kh.at[step, 1 - side],
                      k_send.at[step, side], k_recv.at[step, 1 - side], "lev", side)

    @pl.loop(0, chunks)
    def _(chunk):
        for side in (0, 1):
            j_copy(0, side, chunk).start()

    for side in (0, 1):
        i_copy(0, side).start()
    load_f = pltpu.make_async_copy(f_in, even.at[:, pl.ds(1, I)], load_sems.at[0])
    load_c = pltpu.make_async_copy(c_in, crowd, load_sems.at[1])
    load_f.start()
    load_c.start()
    load_f.wait()

    @pl.loop(0, I)
    def _(i):
        for j in range(J):
            kf[0, 0, j, pl.ds(i, 1), :] = even[j, i + 1, 0:1, :]
            kf[0, 1, j, pl.ds(i, 1), :] = even[j, i + 1, K - 1:K, :]

    load_c.wait()
    for side in (0, 1):
        k_copy(0, side).start()

    def out_copy(chunk):
        here = pl.ds(chunk * rows, rows)
        return pltpu.make_async_copy(
            fields[STEPS % 2].at[:, pl.ds(1 + chunk * rows, rows)], out.at[:, here],
            out_sems.at[chunk])

    at_k = lax.broadcasted_iota(jnp.int32, (K, L), 0)

    for step in range(STEPS):
        source, target = fields[step % 2], fields[(step + 1) % 2]
        last = step == STEPS - 1
        for side in (0, 1):
            i_copy(step, side).wait_recv()
            k_copy(step, side).wait_recv()
            if step >= 1:
                i_copy(step - 1, side).wait_send()

        def send_on(chunk):
            if last:
                out_copy(chunk).start()
            else:
                for side in (0, 1):
                    j_copy(step + 1, side, chunk).start()

        @pl.loop(0, chunks)
        def _(chunk):
            for side in (0, 1):
                j_copy(step, side, chunk).wait_recv()
                if step >= 1:
                    j_copy(step - 1, side, chunk).wait_send()

            @pl.loop(0, rows)
            def _(row):
                i = chunk * rows + row
                for j in range(J):
                    middle = source[j, i + 1]
                    below = jh[step, 0, i] if j == 0 else source[j - 1, i + 1]
                    above = jh[step, 1, i] if j == J - 1 else source[j + 1, i + 1]
                    total = below + above + source[j, i] + source[j, i + 2]
                    total += jnp.where(at_k == 0, kh[step, 0, j, pl.ds(i, 1), :],
                                       pltpu.roll(middle, 1, 0))
                    total += jnp.where(at_k == K - 1, kh[step, 1, j, pl.ds(i, 1), :],
                                       pltpu.roll(middle, K - 1, 0))
                    new = middle * (0.6 - 0.2 * (middle * crowd[j, i])) + 0.1 * total
                    target[j, i + 1] = new
                    if not last:
                        kf[step + 1, 0, j, pl.ds(i, 1), :] = new[0:1]
                        kf[step + 1, 1, j, pl.ds(i, 1), :] = new[K - 1:K]

            @pl.when(chunk > 0)
            def _():
                send_on(chunk - 1)

        send_on(chunks - 1)
        if not last:
            for side in (0, 1):
                i_copy(step + 1, side).start()
                k_copy(step + 1, side).start()

    for side in (0, 1):
        i_copy(STEPS - 1, side).wait_send()
        for step in range(STEPS):
            k_copy(step, side).wait_send()

    @pl.loop(0, chunks)
    def _(chunk):
        for side in (0, 1):
            j_copy(STEPS - 1, side, chunk).wait_send()
        out_copy(chunk).wait()


def local(sizes, field_values, crowding):
    J, I, K, L = shape = field_values.shape
    rows = math.gcd(I, CHUNK_ROWS)
    chunks = I // rows
    dtype = field_values.dtype
    DMA = pltpu.SemaphoreType.DMA
    return pl.pallas_call(
        functools.partial(march_kernel, sizes, shape, rows),
        out_shape=jax.ShapeDtypeStruct(shape, dtype),
        in_specs=[pl.BlockSpec(memory_space=pl.ANY)] * 2,
        out_specs=pl.BlockSpec(memory_space=pl.ANY),
        scratch_shapes=[
            pltpu.VMEM((J, I + 2, K, L), dtype),
            pltpu.VMEM((J, I + 2, K, L), dtype),
            pltpu.VMEM(shape, dtype),
            pltpu.VMEM((STEPS, 2, I, K, L), dtype),
            pltpu.VMEM((STEPS, 2, J, I, L), dtype),
            pltpu.VMEM((STEPS, 2, J, I, L), dtype),
            DMA((2,)),
            DMA((STEPS, 2, chunks)),
            DMA((STEPS, 2, chunks)),
            DMA((STEPS, 2)),
            DMA((STEPS, 2)),
            DMA((STEPS, 2)),
            DMA((STEPS, 2)),
            DMA((chunks,)),
        ],
        compiler_params=pltpu.CompilerParams(
            collective_id=0, has_side_effects=True, vmem_limit_bytes=67043328),
    )(field_values, crowding)


def solution(mesh):
    spec = P("lat", "lon", "lev", None)
    sizes = tuple(mesh.shape[axis] for axis in AXES)
    return jax.shard_map(
        functools.partial(local, sizes), mesh=mesh, in_specs=(spec, spec), out_specs=spec,
        check_vma=False,
    )
```

time: 624 us -> 427 us (0.68)
  waiting for transfers between devices: 431 us -> 0 us
  Pallas kernels: 0 us -> 416 us
  other arithmetic: 136 us -> 0 us
  starting transfers between devices: 23.4 us -> 0 us
  local copies, waits for them, and re-layouts: 33.5 us -> 10.6 us
    ppermute x18 -> x0, waiting for transfers between devices: 431 us -> none  [the longest x9 230 us: padded_2(): lax.ppermute(lax.slice_in_dim(block, block.shape[dim] - width, None, axis...]
    pallas_call x0 -> x1, Pallas kernels: none -> 416 us  [local(): pl.pallas_call(functools.partial(march_kernel, sizes, shape, rows), out_s...]
    add x3 -> x0, other arithmetic: 133 us -> none  [march_step(): return middle + 0.1 * spread + 0.2 * middle * (1.0 - middle * crowding)]
    ppermute x18 -> x0, starting transfers between devices: 23.4 us -> none  [the longest x9 12.1 us: padded_2(): lax.ppermute(lax.slice_in_dim(block, 0, width, axis=dim), axis, backward)]
    slice x10 -> x0, local copies, waits for them, and re-layouts: 13.1 us -> none  [the longest x6 8.14 us: padded_2(): lax.slice_in_dim(block, block.shape[dim] - width, None, axis=dim)]
    unnamed x18 -> x1, local copies, waits for them, and re-layouts: 13 us -> 10.6 us
  transfers between devices with their start and end apart: 18 -> 0, of which waited for: 15 -> 0; matrix products, arithmetic and copies ran while one was open for 2% -> 0% of each run, Pallas kernels for 0% -> 0%
where the time goes in v1:
time: 427 us
  Pallas kernels  416 us (97%)
  local copies, waits for them, and re-layouts  10.6 us (2%)
    pallas_call x1, Pallas kernels, local(): pl.pallas_call(functools.partial(march_kernel, sizes, shape, rows), out_s...  416 us
    unnamed x1, local copies, waits for them, and re-layouts  10.6 us

profile of v1, /device:TPU:0, one launch (start us, length us, event | category | flops | bytes accessed | tf_op | source)
XLA Modules:
  0.0 426.9 jit_solution(12747970159761404137)
XLA Ops:
  0.0 416.3 %shard_map.28 = f32[4,64,96,128]{3,2,1,0:T(8,128)} custom-call(f32[4,64,96,128]{3,2,1,0:T(8,128)} %f_in.1, f32[4,64,96,128]{3,2,1,0:T(8,128)} %c_in.1), custom_call_target="tpu_custom_call" | custom-call | tf_op jit(solution)/shard_map/pallas_call | solution.py:160
  416.3 10.6 %copy.4 = f32[4,64,96,128]{3,2,1,0:T(8,128)} copy(f32[4,64,96,128]{3,2,1,0:T(8,128)} %shard_map.28) | data formatting | bytes 25165824

commit v2 on v1

--- a/solution.py
+++ b/solution.py
@@ -10,12 +10,13 @@
 
 STEPS = 3
 CHUNK_ROWS = 8
+WINDOW = 3
 MESH = pl.DeviceIdType.MESH
 AXES = ("lat", "lon", "lev")
 
 
-def march_kernel(sizes, shape, rows, f_in, c_in, out, even, odd, crowd, jh, kh, kf,
-                 load_sems, j_send, j_recv, i_send, i_recv, k_send, k_recv, out_sems):
+def march_kernel(sizes, shape, rows, f_in, c_in, odd, even, crowd, jh, kh, kf,
+                 load_sems, j_send, j_recv, i_send, i_recv, k_send, k_recv):
     J, I, K, L = shape
     chunks = I // rows
     near = {}
@@ -57,7 +58,9 @@
         return remote(kf.at[step, side], kh.at[step, 1 - side],
                       k_send.at[step, side], k_recv.at[step, 1 - side], "lev", side)
 
-    @pl.loop(0, chunks)
+    window = min(WINDOW, chunks - 1)
+
+    @pl.loop(0, window)
     def _(chunk):
         for side in (0, 1):
             j_copy(0, side, chunk).start()
@@ -80,12 +83,6 @@
     for side in (0, 1):
         k_copy(0, side).start()
 
-    def out_copy(chunk):
-        here = pl.ds(chunk * rows, rows)
-        return pltpu.make_async_copy(
-            fields[STEPS % 2].at[:, pl.ds(1 + chunk * rows, rows)], out.at[:, here],
-            out_sems.at[chunk])
-
     at_k = lax.broadcasted_iota(jnp.int32, (K, L), 0)
 
     for step in range(STEPS):
@@ -97,19 +94,22 @@
             if step >= 1:
                 i_copy(step - 1, side).wait_send()
 
-        def send_on(chunk):
-            if last:
-                out_copy(chunk).start()
-            else:
-                for side in (0, 1):
-                    j_copy(step + 1, side, chunk).start()
-
         @pl.loop(0, chunks)
         def _(chunk):
             for side in (0, 1):
                 j_copy(step, side, chunk).wait_recv()
-                if step >= 1:
-                    j_copy(step - 1, side, chunk).wait_send()
+                j_copy(step, side, chunk).wait_send()
+
+            @pl.when(chunk + window < chunks)
+            def _():
+                for side in (0, 1):
+                    j_copy(step, side, chunk + window).start()
+
+            if not last:
+                @pl.when(chunk + window >= chunks)
+                def _():
+                    for side in (0, 1):
+                        j_copy(step + 1, side, chunk + window - chunks).start()
 
             @pl.loop(0, rows)
             def _(row):
@@ -129,11 +129,6 @@
                         kf[step + 1, 0, j, pl.ds(i, 1), :] = new[0:1]
                         kf[step + 1, 1, j, pl.ds(i, 1), :] = new[K - 1:K]
 
-            @pl.when(chunk > 0)
-            def _():
-                send_on(chunk - 1)
-
-        send_on(chunks - 1)
         if not last:
             for side in (0, 1):
                 i_copy(step + 1, side).start()
@@ -144,11 +139,15 @@
         for step in range(STEPS):
             k_copy(step, side).wait_send()
 
-    @pl.loop(0, chunks)
-    def _(chunk):
-        for side in (0, 1):
-            j_copy(STEPS - 1, side, chunk).wait_send()
-        out_copy(chunk).wait()
+
+def write_kernel(shape, held, out, sems):
+    J, I = shape[:2]
+    copies = [pltpu.make_async_copy(held.at[j, pl.ds(1, I)], out.at[j], sems.at[j])
+              for j in range(J)]
+    for copy in copies:
+        copy.start()
+    for copy in copies:
+        copy.wait()
 
 
 def local(sizes, field_values, crowding):
@@ -157,13 +156,12 @@
     chunks = I // rows
     dtype = field_values.dtype
     DMA = pltpu.SemaphoreType.DMA
-    return pl.pallas_call(
+    marched = pl.pallas_call(
         functools.partial(march_kernel, sizes, shape, rows),
-        out_shape=jax.ShapeDtypeStruct(shape, dtype),
+        out_shape=pltpu.VMEM((J, I + 2, K, L), dtype),
         in_specs=[pl.BlockSpec(memory_space=pl.ANY)] * 2,
-        out_specs=pl.BlockSpec(memory_space=pl.ANY),
+        out_specs=pl.BlockSpec(memory_space=pltpu.VMEM),
         scratch_shapes=[
-            pltpu.VMEM((J, I + 2, K, L), dtype),
             pltpu.VMEM((J, I + 2, K, L), dtype),
             pltpu.VMEM(shape, dtype),
             pltpu.VMEM((STEPS, 2, I, K, L), dtype),
@@ -176,11 +174,18 @@
             DMA((STEPS, 2)),
             DMA((STEPS, 2)),
             DMA((STEPS, 2)),
-            DMA((chunks,)),
         ],
         compiler_params=pltpu.CompilerParams(
-            collective_id=0, has_side_effects=True, vmem_limit_bytes=67043328),
+            collective_id=0, has_side_effects=True, vmem_limit_bytes=50 * 1024 * 1024),
     )(field_values, crowding)
+    return pl.pallas_call(
+        functools.partial(write_kernel, shape),
+        out_shape=jax.ShapeDtypeStruct(shape, dtype),
+        in_specs=[pl.BlockSpec(memory_space=pltpu.VMEM)],
+        out_specs=pl.BlockSpec(memory_space=pl.ANY),
+        scratch_shapes=[DMA((J,))],
+        compiler_params=pltpu.CompilerParams(vmem_limit_bytes=1024 * 1024),
+    )(pltpu.with_memory_space_constraint(marched, pltpu.VMEM))
 
 
 def solution(mesh):

time: 427 us -> 419 us (0.981)
  local copies, waits for them, and re-layouts: 10.6 us -> 0 us
    unnamed x1 -> x0, local copies, waits for them, and re-layouts: 10.6 us -> none
    pallas_call x0 -> x1, Pallas kernels: none -> 4.72 us  [local(): pl.pallas_call(functools.partial(write_kernel, shape), out_shape=jax.Shap...]
where the time goes in v2:
time: 419 us
  Pallas kernels  419 us (100%)
    pallas_call x1, Pallas kernels, local(): pl.pallas_call(functools.partial(march_kernel, sizes, shape, rows), out_s...  415 us

profile of v2, /device:TPU:0, one launch (start us, length us, event | category | flops | bytes accessed | tf_op | source)
XLA Modules:
  0.0 419.3 jit_solution(3191463610524947937)
XLA Ops:
  0.0 414.5 %shard_map.28.held = f32[4,66,96,128]{3,2,1,0:T(8,128)S(1)} custom-call(f32[4,64,96,128]{3,2,1,0:T(8,128)} %f_in.1, f32[4,64,96,128]{3,2,1,0:T(8,128)} %c_in.1), custom_call_target="tpu_custom_call" | custom-call | tf_op jit(solution)/shard_map/pallas_call | solution.py:159
  414.5 4.7 %shard_map.29 = f32[4,64,96,128]{3,2,1,0:T(8,128)} custom-call(f32[4,66,96,128]{3,2,1,0:T(8,128)S(1)} %shard_map.28.held), custom_call_target="tpu_custom_call" | custom-call | tf_op jit(solution)/shard_map/pallas_call | solution.py:181
